TPU v7x, 128 devices: a whole 4x4x4 slice. The times are simulated.
128 devices in a mesh: head: 16 (over z, y), batch: 8 (over x, core).
Axes of the slice: x: 4, y: 4, z: 4, core: 2. Of those that a mesh axis runs over, the one named last changes fastest.
Arguments:
- incoming_hidden_stream: bfloat16 [1024, 4096], P('batch'), may hold values from -6 to 6
- reception_projection: bfloat16 [4096, 4096], P(None, 'head'), may hold values from -0.09375 to 0.09375
- address_projection: bfloat16 [4096, 4096], P(None, 'head'), may hold values from -0.09375 to 0.09375
- payload_projection: bfloat16 [4096, 4096], P(None, 'head'), may hold values from -0.09375 to 0.09375
- sigmoid_filter_matrix: bfloat16 [4096, 4096], P(None, 'head'), may hold values from -0.09375 to 0.09375
- forgetting_speed: float32 [1024, 4096], P('batch', 'head'), may hold values from 0.01 to 1.5
- adaptation_step_size: float32 [1024, 4096], P('batch', 'head'), may hold values from 0 to 1
- diagonal_boost: float32 [4096], P('head'), may hold values from -0.6 to 0.6
- subspace_standardize_scale: float32 [4096], P('head'), may hold values from 0.5 to 2
- recurrent_memory_matrix: float32 [128, 64, 64, 64], P('batch', 'head'), may hold values from -6 to 6
- emission_projection: bfloat16 [4096, 4096], P('head'), may hold values from -0.09375 to 0.09375
- closing_standardize_scale: float32 [4096], replicated, may hold values from 0.7 to 2
- lexicon_projection: bfloat16 [4096, 65536], P(None, ('head', 'batch')), may hold values from -32 to 32
- proposed_tokens_list: int32 [128, 8], P('batch'), may hold values from 0 to 65535
- threshold_milli_nats: int32 [128, 8], P('batch'), may hold values from -22000 to -10001
Outputs:
- new_state: float32 [128, 64, 64, 64], P('batch', 'head')
- margin: float32 [128, 8], P('batch')
- accept: float32 [128, 8], P('batch')
All inputs are finite; a program needn't handle non-finite values.
Results may differ from a plain program's by a relative error of at most 0.0017.
Values may be sent and summed in bfloat16 or wider, within the bound.
A program may use at most 128 MiB of HBM per device.

v0:
```python
import math
import jax
import jax.numpy as jnp
from jax import lax
from jax.sharding import Mesh
from jax.sharding import PartitionSpec as P

HEAD = ("head_0", "head_1")
HEAD_BATCH = ("head_0", "head_1", "batch")


def in_blocks(x, dim, size):
    before, after = (x.shape[:dim], x.shape[dim + 1 :])
    return jnp.moveaxis(x.reshape(*before, size, -1, *after), dim, 0)


def sent_and_summed(x, axis, dim):
    size = lax.axis_size(axis)
    parts = lax.all_to_all(in_blocks(x, dim, size), axis, 0, 0, tiled=True)
    return jnp.sum(parts, axis=0)


def by_axis(x, axes):
    for axis in axes:
        x = lax.psum(x, axis)
    return x


def joined_along(parts, dim):
    parts = jnp.moveaxis(parts, 0, dim)
    shape = parts.shape
    return parts.reshape(*shape[:dim], shape[dim] * shape[dim + 1], *shape[dim + 2 :])


def sent_to_all(x, axis):
    copies = jnp.broadcast_to(x, (lax.axis_size(axis), *x.shape))
    return lax.all_to_all(copies, axis, split_axis=0, concat_axis=0, tiled=True)


def gathered_copies(x, axis, dim):
    return joined_along(sent_to_all(x, axis), dim)


def gathered_once(x, axis):
    leaves = jax.tree.leaves(x)
    sequence = sorted(range(len(leaves)), key=lambda k: -leaves[k].size)
    width = (1, *leaves[sequence[0]].shape)[-1]
    lines = [
        jnp.pad(leaves[k].reshape(-1), (0, -leaves[k].size % width)).reshape(-1, width)
        for k in sequence
    ]
    both, at, found = (sent_to_all(jnp.concatenate(lines), axis), 0, {})
    for k, line in zip(sequence, lines):
        share = both[:, at : at + len(line)].reshape(len(both), -1)
        found[k] = share[:, : leaves[k].size].reshape(-1, *leaves[k].shape)
        at += len(line)
    numbers = iter(range(len(leaves)))
    return jax.tree.map(lambda _: found[next(numbers)], x)


def combined_pairwise(pieces, combine):
    while len(jax.tree.leaves(pieces)[0]) > 1:
        pieces = jax.vmap(combine)(
            *(jax.tree.map(lambda part: part[side::2], pieces) for side in (0, 1))
        )
    return jax.tree.map(lambda part: part[0], pieces)


def combined_all(x, axis, combine):
    pieces = gathered_once(x, axis)
    return combined_pairwise(pieces, combine)


def gathered_by_type(x, axis):
    leaves, found = (jax.tree.leaves(x), {})
    for initial, a in enumerate(leaves):
        if initial not in found:
            alike = [k for k, b in enumerate(leaves) if b.dtype == a.dtype]
            got = (
                gathered_once([leaves[k] for k in alike], axis)
                if len(alike) > 1
                else [sent_to_all(a, axis)]
            )
            for k, b in zip(alike, got):
                found[k] = b
    numbers = iter(range(len(leaves)))
    return jax.tree.map(lambda _: found[next(numbers)], x)


def merged(x, axis, combine):
    pieces = gathered_by_type(x, axis)
    return combined_pairwise(pieces, combine)


def advance(start, reception_vectors, address_vectors, payload_vectors, decay, rate):
    unit = (
        address_vectors
        * lax.rsqrt(jnp.mean(address_vectors * address_vectors, -1, keepdims=True) + 1e-06)
        / math.sqrt(address_vectors.shape[-1])
    )
    inputs = tuple(
        (
            jnp.moveaxis(item, 1, 0)
            for item in (reception_vectors, address_vectors, payload_vectors, decay, unit, rate)
        )
    )

    def step(current, pieces):
        recept_now, keys_now, values_now, decay_now, unit_now, rate_now = pieces
        recall = jnp.einsum("bhij,bhj->bhi", current, unit_now, precision=lax.Precision.HIGHEST)
        current = (
            current * decay_now[:, :, None, :]
            - recall[:, :, :, None] * (unit_now * rate_now)[:, :, None, :]
            + values_now[:, :, :, None] * keys_now[:, :, None, :]
        )
        output = jnp.einsum("bhij,bhj->bhi", current, recept_now, precision=lax.Precision.HIGHEST)
        return (current, output)

    final, outputs = lax.scan(step, start, inputs)
    return (final, jnp.moveaxis(outputs, 0, 1))


def combine_stats(first, second):
    top = jnp.maximum(first[0], second[0])
    summed = first[1] * jnp.exp(first[0] - top) + second[1] * jnp.exp(second[0] - top)
    return (top, summed, first[2] + second[2])


def local_stats(logits, ids_flat, offset):
    peak = jnp.max(logits, -1)
    total = jnp.sum(jnp.exp(logits - peak[:, None]), -1)
    column = lax.broadcasted_iota(jnp.int32, logits.shape, 1)
    target = jnp.sum(jnp.where(column == (ids_flat - offset)[:, None], logits, 0.0), -1)
    return (peak, total, target)


def shards(
    incoming_hidden_stream,
    reception_projection,
    address_projection,
    payload_projection,
    sigmoid_filter_matrix,
    forgetting_speed,
    adaptation_step_size,
    diagonal_boost,
    subspace_standardize_scale,
    recurrent_memory_matrix,
    emission_projection,
    closing_standardize_scale,
    lexicon_projection,
    proposed_tokens_list,
    threshold_milli_nats,
):
    seq_dev, draft_len = proposed_tokens_list.shape
    lanes_on_shard, subspace_size = (
        recurrent_memory_matrix.shape[1],
        recurrent_memory_matrix.shape[2],
    )
    tok_dev = seq_dev * draft_len
    width = incoming_hidden_stream.shape[1]
    shape4 = (seq_dev, draft_len, lanes_on_shard, subspace_size)
    reception_vectors = jnp.dot(
        incoming_hidden_stream, reception_projection, preferred_element_type=jnp.float32
    ).reshape(shape4)
    address_vectors = jnp.dot(
        incoming_hidden_stream, address_projection, preferred_element_type=jnp.float32
    ).reshape(shape4)
    payload_vectors = jnp.dot(
        incoming_hidden_stream, payload_projection, preferred_element_type=jnp.float32
    ).reshape(shape4)
    gate = jnp.dot(
        incoming_hidden_stream, sigmoid_filter_matrix, preferred_element_type=jnp.float32
    )
    decay = jnp.exp(-forgetting_speed).reshape(shape4)
    rate = adaptation_step_size.reshape(shape4)
    new_state, wkv = advance(
        recurrent_memory_matrix, reception_vectors, address_vectors, payload_vectors, decay, rate
    )
    center = wkv - jnp.mean(wkv, -1, keepdims=True)
    interpolated_embedding = (
        center
        * lax.rsqrt(jnp.mean(center * center, -1, keepdims=True) + 1e-05)
        * subspace_standardize_scale.reshape(lanes_on_shard, subspace_size)
    )
    interpolated_embedding = (
        interpolated_embedding
        + jnp.sum(
            reception_vectors
            * address_vectors
            * diagonal_boost.reshape(lanes_on_shard, subspace_size),
            -1,
            keepdims=True,
        )
        * payload_vectors
    )
    gated = (
        interpolated_embedding.reshape(tok_dev, lanes_on_shard * subspace_size)
        * jax.nn.sigmoid(gate)
    ).astype(jnp.bfloat16)
    partial_out = jnp.dot(gated, emission_projection, preferred_element_type=jnp.float32)
    share = sent_and_summed(partial_out, HEAD, 1)
    cols = share.shape[1]
    begin = lax.axis_index(HEAD) * cols
    residual = (
        lax.dynamic_slice_in_dim(incoming_hidden_stream, begin, cols, 1).astype(jnp.float32) + share
    )
    moment_one, moment_two = (
        by_axis(jnp.sum(residual, -1), HEAD),
        by_axis(jnp.sum(residual * residual, -1), HEAD),
    )
    mean_row = moment_one / width
    variance = moment_two / width - mean_row * mean_row
    gain_part = lax.dynamic_slice_in_dim(closing_standardize_scale, begin, cols, 0)
    normed_part = (
        (residual - mean_row[:, None]) * lax.rsqrt(variance + 1e-05)[:, None] * gain_part
    ).astype(jnp.bfloat16)
    normed = gathered_copies(normed_part, HEAD, 1)
    every, every_ids = (
        lax.all_gather(normed, "batch", axis=0, tiled=True),
        lax.all_gather(proposed_tokens_list, "batch", axis=0, tiled=True),
    )
    logits = jnp.dot(every, lexicon_projection, preferred_element_type=jnp.float32)
    vcols = lexicon_projection.shape[1]
    offset = (lax.axis_index(HEAD) * lax.axis_size("batch") + lax.axis_index("batch")) * vcols
    peak, total, target = local_stats(logits, every_ids.reshape(-1), offset)
    peak, total, target = combined_all((peak, total, target), "batch", combine_stats)
    row_begin = lax.axis_index("batch") * tok_dev
    peak = lax.dynamic_slice_in_dim(peak, row_begin, tok_dev, 0)
    total = lax.dynamic_slice_in_dim(total, row_begin, tok_dev, 0)
    target = lax.dynamic_slice_in_dim(target, row_begin, tok_dev, 0)
    top, summed, target = merged((peak, total, target), HEAD, combine_stats)
    logprob = target - (top + jnp.log(summed))
    margin = logprob.reshape(seq_dev, draft_len) - threshold_milli_nats.astype(jnp.float32) / 1000.0
    accept = jnp.cumprod(jax.nn.sigmoid(margin * 0.5), axis=1)
    return (new_state, margin, accept)


def solution(mesh):
    split = Mesh(mesh.devices.reshape(4, 4, mesh.shape["batch"]), ("head_0", "head_1", "batch"))
    return jax.shard_map(
        shards,
        mesh=split,
        in_specs=(
            P("batch", None),
            P(None, HEAD),
            P(None, HEAD),
            P(None, HEAD),
            P(None, HEAD),
            P("batch", HEAD),
            P("batch", HEAD),
            P(HEAD),
            P(HEAD),
            P("batch", HEAD, None, None),
            P(HEAD, None),
            P(),
            P(None, HEAD_BATCH),
            P("batch", None),
            P("batch", None),
        ),
        out_specs=(P("batch", HEAD, None, None), P("batch", None), P("batch", None)),
        check_vma=False,
    )
```

profile of v0, /device:TPU:0, one launch (start us, length us, event | category | flops | bytes accessed | tf_op | source)
XLA Modules:
  0.0 318.9 jit_solution(11417522193714851282)
XLA Ops:
  7.2 3.3 %copy.146 = f32[16,4,64,64]{3,2,1,0:T(8,128)} copy(f32[16,4,64,64]{3,2,1,0:T(8,128)} %param.26) | data formatting | bytes 2097152
  29.0 105.4 %while.12 = (s32[]{:T(128)}, f32[16,4,64,64]{3,2,1,0:T(8,128)}, f32[8,16,4,64]{3,2,1,0:T(4,128)S(1)}, f32[8,16,4,64]{3,2,0,1:T(4,128)}, f32[8,16,4,64]{3,2,1,0:T...) while((s32[]{:T(128)}, f32[16,4,64,64]{3,2,1,0:T(8,128)}, ...), condition=%wide.region_2.3_spmd, body=%wide.region_1.2_spmd.sunk | while | flops 7606274 | bytes 13009081 | solution.py:119
  31.5 4.9 %fusion.54 = f32[16,4,1,64]{3,2,1,0:T(1,128)S(1)} fusion(f32[16,4,64,1]{2,3,1,0:T(1,128)S(1)} %bitcast.118, f32[16,4,64,64]{3,2,1,0:T(8,128)} %get-tuple-element.245), kind=kOutput, calls=%fused_computation.79.clone.1 | convolution fusion | flops 3145728 | bytes 1081344 | tf_op jit(solution)/shard_map/while/body/eval_jaxpr/bhij,bhj->bhi/dot_general | solution.py:110
  38.8 3.3 %fusion.55 = f32[16,4,1,64]{3,2,1,0:T(1,128)S(1)} fusion(f32[16,4,64,64]{3,2,1,0:T(8,128)S(1)} %multiply_add_fusion.8, f32[16,4,64,1]{2,3,1,0:T(1,128)S(1)} %bitcast.117), kind=kOutput, calls=%fused_computation.80.clone.1 | convolution fusion | flops 3145728 | bytes 1081344 | tf_op jit(solution)/shard_map/while/body/eval_jaxpr/bhij,bhj->bhi/dot_general | solution.py:116
  44.7 4.9 %fusion.54 = f32[16,4,1,64]{3,2,1,0:T(1,128)S(1)} fusion(f32[16,4,64,1]{2,3,1,0:T(1,128)S(1)} %bitcast.118, f32[16,4,64,64]{3,2,1,0:T(8,128)} %get-tuple-element.245), kind=kOutput, calls=%fused_computation.79.clone.1 | convolution fusion | flops 3145728 | bytes 1081344 | tf_op jit(solution)/shard_map/while/body/eval_jaxpr/bhij,bhj->bhi/dot_general | solution.py:110
  52.0 3.3 %fusion.55 = f32[16,4,1,64]{3,2,1,0:T(1,128)S(1)} fusion(f32[16,4,64,64]{3,2,1,0:T(8,128)S(1)} %multiply_add_fusion.8, f32[16,4,64,1]{2,3,1,0:T(1,128)S(1)} %bitcast.117), kind=kOutput, calls=%fused_computation.80.clone.1 | convolution fusion | flops 3145728 | bytes 1081344 | tf_op jit(solution)/shard_map/while/body/eval_jaxpr/bhij,bhj->bhi/dot_general | solution.py:116
  57.9 4.9 %fusion.54 = f32[16,4,1,64]{3,2,1,0:T(1,128)S(1)} fusion(f32[16,4,64,1]{2,3,1,0:T(1,128)S(1)} %bitcast.118, f32[16,4,64,64]{3,2,1,0:T(8,128)} %get-tuple-element.245), kind=kOutput, calls=%fused_computation.79.clone.1 | convolution fusion | flops 3145728 | bytes 1081344 | tf_op jit(solution)/shard_map/while/body/eval_jaxpr/bhij,bhj->bhi/dot_general | solution.py:110
  65.1 3.3 %fusion.55 = f32[16,4,1,64]{3,2,1,0:T(1,128)S(1)} fusion(f32[16,4,64,64]{3,2,1,0:T(8,128)S(1)} %multiply_add_fusion.8, f32[16,4,64,1]{2,3,1,0:T(1,128)S(1)} %bitcast.117), kind=kOutput, calls=%fused_computation.80.clone.1 | convolution fusion | flops 3145728 | bytes 1081344 | tf_op jit(solution)/shard_map/while/body/eval_jaxpr/bhij,bhj->bhi/dot_general | solution.py:116
  71.0 4.9 %fusion.54 = f32[16,4,1,64]{3,2,1,0:T(1,128)S(1)} fusion(f32[16,4,64,1]{2,3,1,0:T(1,128)S(1)} %bitcast.118, f32[16,4,64,64]{3,2,1,0:T(8,128)} %get-tuple-element.245), kind=kOutput, calls=%fused_computation.79.clone.1 | convolution fusion | flops 3145728 | bytes 1081344 | tf_op jit(solution)/shard_map/while/body/eval_jaxpr/bhij,bhj->bhi/dot_general | solution.py:110
  78.3 3.3 %fusion.55 = f32[16,4,1,64]{3,2,1,0:T(1,128)S(1)} fusion(f32[16,4,64,64]{3,2,1,0:T(8,128)S(1)} %multiply_add_fusion.8, f32[16,4,64,1]{2,3,1,0:T(1,128)S(1)} %bitcast.117), kind=kOutput, calls=%fused_computation.80.clone.1 | convolution fusion | flops 3145728 | bytes 1081344 | tf_op jit(solution)/shard_map/while/body/eval_jaxpr/bhij,bhj->bhi/dot_general | solution.py:116
  84.2 4.9 %fusion.54 = f32[16,4,1,64]{3,2,1,0:T(1,128)S(1)} fusion(f32[16,4,64,1]{2,3,1,0:T(1,128)S(1)} %bitcast.118, f32[16,4,64,64]{3,2,1,0:T(8,128)} %get-tuple-element.245), kind=kOutput, calls=%fused_computation.79.clone.1 | convolution fusion | flops 3145728 | bytes 1081344 | tf_op jit(solution)/shard_map/while/body/eval_jaxpr/bhij,bhj->bhi/dot_general | solution.py:110
  91.5 3.3 %fusion.55 = f32[16,4,1,64]{3,2,1,0:T(1,128)S(1)} fusion(f32[16,4,64,64]{3,2,1,0:T(8,128)S(1)} %multiply_add_fusion.8, f32[16,4,64,1]{2,3,1,0:T(1,128)S(1)} %bitcast.117), kind=kOutput, calls=%fused_computation.80.clone.1 | convolution fusion | flops 3145728 | bytes 1081344 | tf_op jit(solution)/shard_map/while/body/eval_jaxpr/bhij,bhj->bhi/dot_general | solution.py:116
  97.4 4.9 %fusion.54 = f32[16,4,1,64]{3,2,1,0:T(1,128)S(1)} fusion(f32[16,4,64,1]{2,3,1,0:T(1,128)S(1)} %bitcast.118, f32[16,4,64,64]{3,2,1,0:T(8,128)} %get-tuple-element.245), kind=kOutput, calls=%fused_computation.79.clone.1 | convolution fusion | flops 3145728 | bytes 1081344 | tf_op jit(solution)/shard_map/while/body/eval_jaxpr/bhij,bhj->bhi/dot_general | solution.py:110
  104.7 3.3 %fusion.55 = f32[16,4,1,64]{3,2,1,0:T(1,128)S(1)} fusion(f32[16,4,64,64]{3,2,1,0:T(8,128)S(1)} %multiply_add_fusion.8, f32[16,4,64,1]{2,3,1,0:T(1,128)S(1)} %bitcast.117), kind=kOutput, calls=%fused_computation.80.clone.1 | convolution fusion | flops 3145728 | bytes 1081344 | tf_op jit(solution)/shard_map/while/body/eval_jaxpr/bhij,bhj->bhi/dot_general | solution.py:116
  110.6 4.9 %fusion.54 = f32[16,4,1,64]{3,2,1,0:T(1,128)S(1)} fusion(f32[16,4,64,1]{2,3,1,0:T(1,128)S(1)} %bitcast.118, f32[16,4,64,64]{3,2,1,0:T(8,128)} %get-tuple-element.245), kind=kOutput, calls=%fused_computation.79.clone.1 | convolution fusion | flops 3145728 | bytes 1081344 | tf_op jit(solution)/shard_map/while/body/eval_jaxpr/bhij,bhj->bhi/dot_general | solution.py:110
  117.9 3.3 %fusion.55 = f32[16,4,1,64]{3,2,1,0:T(1,128)S(1)} fusion(f32[16,4,64,64]{3,2,1,0:T(8,128)S(1)} %multiply_add_fusion.8, f32[16,4,64,1]{2,3,1,0:T(1,128)S(1)} %bitcast.117), kind=kOutput, calls=%fused_computation.80.clone.1 | convolution fusion | flops 3145728 | bytes 1081344 | tf_op jit(solution)/shard_map/while/body/eval_jaxpr/bhij,bhj->bhi/dot_general | solution.py:116
  123.8 4.9 %fusion.54 = f32[16,4,1,64]{3,2,1,0:T(1,128)S(1)} fusion(f32[16,4,64,1]{2,3,1,0:T(1,128)S(1)} %bitcast.118, f32[16,4,64,64]{3,2,1,0:T(8,128)} %get-tuple-element.245), kind=kOutput, calls=%fused_computation.79.clone.1 | convolution fusion | flops 3145728 | bytes 1081344 | tf_op jit(solution)/shard_map/while/body/eval_jaxpr/bhij,bhj->bhi/dot_general | solution.py:110
  131.1 3.3 %fusion.55 = f32[16,4,1,64]{3,2,1,0:T(1,128)S(1)} fusion(f32[16,4,64,64]{3,2,1,0:T(8,128)S(1)} %multiply_add_fusion.8, f32[16,4,64,1]{2,3,1,0:T(1,128)S(1)} %bitcast.117), kind=kOutput, calls=%fused_computation.80.clone.1 | convolution fusion | flops 3145728 | bytes 1081344 | tf_op jit(solution)/shard_map/while/body/eval_jaxpr/bhij,bhj->bhi/dot_general | solution.py:116
  139.9 4.2 %fusion.5 = f32[128,4096]{1,0:T(8,128)} fusion(bf16[256,4096]{1,0:T(8,128)(2,1)S(1)} %copy-done, f32[128,256]{1,0:T(8,128)S(1)} %reshape.129, bf16[128,4096]{1,0:T(8,128)(2,1)S(1)} %copy-done.3, bf16[4096,256]{1,0:T(8,128)(2,1)} %param.21), kind=kOutput, calls=%fused_computation.18 | convolution fusion | flops 537034752 | bytes 7471104 | tf_op jit(solution)/shard_map/dot_general | solution.py:200
  144.2 3.2 copy.131
  147.3 8.2 %all-to-all-start = ((f32[16,128,256]{2,1,0:T(8,128)}), f32[16,128,256]{2,1,0:T(8,128)}, u32[]{:S(2)}, u32[]{:S(2)}) async-start(f32[16,128,256]{2,1,0:T(8,128)} %bitcast.113), calls=%async_computation | async-start | bytes 4194304 | tf_op jit(solution)/shard_map/all_to_all | solution.py:19
  156.4 31.0 %all-to-all-done = f32[16,128,256]{2,1,0:T(8,128)} async-done(((f32[16,128,256]{2,1,0:T(8,128)}), f32[16,128,256]{2,1,0:T(8,128)}, u32[]{:S(2)}, u32[]{:S(2)}) %all-to-all-start) | async-done | bytes 2097184 | tf_op jit(solution)/shard_map/all_to_all | solution.py:19
  189.2 9.5 %all-reduce.1 = (f32[128]{0:T(128)S(1)}, f32[128]{0:T(128)S(1)}) all-reduce(f32[128]{0:T(128)S(1)} %get-tuple-element.107, f32[128]{0:T(128)S(1)} %get-tuple-element.106), channel_id=1, replica_groups=mesh['head_0'=4,'head_1'=4,'batch'=8] {'head_0'}, use_global_device_ids=true, to_apply=%region_11.12 | all-reduce | flops 256 | bytes 2048 | tf_op jit(solution)/shard_map/psum | solution.py:25
  198.7 7.7 %all-reduce = (f32[128]{0:T(128)S(1)}, f32[128]{0:T(128)S(1)}) all-reduce(f32[128]{0:T(128)S(1)} %get-tuple-element.130, f32[128]{0:T(128)S(1)} %get-tuple-element.131), channel_id=1, replica_groups=mesh['head_0'=4,'head_1'=4,'batch'=8] {'head_1'}, use_global_device_ids=true, to_apply=%region_12.13 | all-reduce | flops 256 | bytes 2048 | tf_op jit(solution)/shard_map/psum | solution.py:25
  206.9 16.6 %all_to_all.20 = bf16[16,128,256]{1,2,0:T(8,128)(2,1)} all-to-all(bf16[16,128,256]{1,2,0:T(8,128)(2,1)S(1)} %broadcast_in_dim.21), channel_id=1, replica_groups=mesh['head_0'=4,'head_1'=4,'batch'=8] {'head_0','head_1'}, dimensions={0} | all-to-all | bytes 2097152 | tf_op jit(solution)/shard_map/all_to_all | solution.py:37
  223.5 13.3 %all-gather = s32[8,16,8]{1,2,0:T(8,128)S(1)} all-gather(s32[1,16,8]{1,2,0:T(8,128)S(1)} %bitcast.136), channel_id=1, replica_groups=mesh['head_0'=4,'head_1'=4,'batch'=8] {'batch'}, dimensions={0}, use_global_device_ids=true | all-gather | bytes 4608 | tf_op jit(solution)/shard_map/all_gather | solution.py:220
  237.0 37.6 %all-gather.3.cloned.1.call-done = bf16[1024,4096]{0,1:T(8,128)(2,1)} async-done(((bf16[128,4096]{0,1:T(8,128)(2,1)}), bf16[1024,4096]{0,1:T(8,128)(2,1)}) %all-gather.3.cloned.1.call-update) | async-done | bytes 8388624 | tf_op jit(solution)/shard_map/all_gather | solution.py:219
  274.6 8.3 %fusion.23 = (f32[1024]{0:T(1024)S(1)}, f32[1024,512]{0,1:T(8,128)S(1)}) fusion(bf16[1024,4096]{0,1:T(8,128)(2,1)} %all-gather.3.cloned.1.call-done, bf16[4096,512]{1,0:T(8,128)(2,1)} %param.29), kind=kOutput, calls=%fused_computation.78 | convolution fusion | flops 4295490560 | bytes 14684160 | tf_op jit(solution)/shard_map/dot_general | solution.py:222
  284.1 4.0 %all-to-all-start.2 = ((f32[8,3,1024]{2,1,0:T(4,128)}), f32[8,3,1024]{2,1,0:T(4,128)S(1)}, u32[]{:S(2)}, u32[]{:S(2)}) async-start(f32[8,3,1024]{2,1,0:T(4,128)} %broadcast_in_dim.23), calls=%async_computation.2 | async-start | bytes 262144 | tf_op jit(solution)/shard_map/all_to_all | solution.py:37
  288.1 6.1 %all-to-all-done.2 = f32[8,3,1024]{2,1,0:T(4,128)S(1)} async-done(((f32[8,3,1024]{2,1,0:T(4,128)}), f32[8,3,1024]{2,1,0:T(4,128)S(1)}, u32[]{:S(2)}, u32[]{:S(2)}) %all-to-all-start.2) | async-done | bytes 98336 | tf_op jit(solution)/shard_map/all_to_all | solution.py:37
  295.4 6.9 %all-to-all-start.3 = ((f32[16,3,128]{2,1,0:T(4,128)}), f32[16,3,128]{2,1,0:T(4,128)S(1)}, u32[]{:S(2)}, u32[]{:S(2)}) async-start(f32[16,3,128]{2,1,0:T(4,128)} %broadcast_in_dim.25), calls=%async_computation.3 | async-start | bytes 65536 | tf_op jit(solution)/shard_map/all_to_all | solution.py:37
  302.5 7.5 %all-to-all-done.3 = f32[16,3,128]{2,1,0:T(4,128)S(1)} async-done(((f32[16,3,128]{2,1,0:T(4,128)}), f32[16,3,128]{2,1,0:T(4,128)S(1)}, u32[]{:S(2)}, u32[]{:S(2)}) %all-to-all-start.3) | async-done | bytes 24608 | tf_op jit(solution)/shard_map/all_to_all | solution.py:37
  (198 shorter events, 70.4 us)
Async XLA Ops:
  7.2 132.8 %copy-start = (bf16[256,4096]{1,0:T(8,128)(2,1)S(1)}, bf16[256,4096]{1,0:T(8,128)(2,1)}, u32[]{:S(2)}) copy-start(bf16[256,4096]{1,0:T(8,128)(2,1)} %param.27) | copy-start | bytes 6291460
  7.2 5.1 %copy-start.3 = (bf16[128,4096]{1,0:T(8,128)(2,1)S(1)}, bf16[128,4096]{1,0:T(8,128)(2,1)}, u32[]{:S(2)}) copy-start(bf16[128,4096]{1,0:T(8,128)(2,1)} %param.17) | copy-start | bytes 3145732
  14.3 3.7 %copy-start.7 = (f32[256]{0:T(256)S(1)}, f32[256]{0:T(256)}, u32[]{:S(2)}) copy-start(f32[256]{0:T(256)} %param.24) | copy-start | bytes 3076
  29.0 105.5 %copy-start.4 = (f32[16,8,4]{2,1,0:T(8,128)S(1)}, f32[16,8,4]{2,1,0:T(8,128)}, u32[]{:S(2)}) copy-start(f32[16,8,4]{2,1,0:T(8,128)} %get-tuple-element.108) | copy-start | bytes 6148
  29.0 106.1 %copy-start.8 = (f32[256]{0:T(256)S(1)}, f32[256]{0:T(256)}, u32[]{:S(2)}) copy-start(f32[256]{0:T(256)} %param.25) | copy-start | bytes 3076
  29.0 8.2 %copy-start.1 = (f32[16,4,64,64]{3,2,1,0:T(8,128)S(1)}, f32[16,4,64,64]{3,2,1,0:T(8,128)}, u32[]{:S(2)}) copy-start(f32[16,4,64,64]{3,2,1,0:T(8,128)} %get-tuple-element.245) | copy-start | bytes 3145732 | tf_op jit(solution)/shard_map/while
  38.8 3.4 %copy-start.2 = (f32[16,4,64,64]{3,2,1,0:T(8,128)}, f32[16,4,64,64]{3,2,1,0:T(8,128)S(1)}, u32[]{:S(2)}) copy-start(f32[16,4,64,64]{3,2,1,0:T(8,128)S(1)} %multiply_add_fusion.8) | copy-start | bytes 3145732 | tf_op jit(solution)/shard_map/while
  42.2 8.2 %copy-start.1 = (f32[16,4,64,64]{3,2,1,0:T(8,128)S(1)}, f32[16,4,64,64]{3,2,1,0:T(8,128)}, u32[]{:S(2)}) copy-start(f32[16,4,64,64]{3,2,1,0:T(8,128)} %get-tuple-element.245) | copy-start | bytes 3145732 | tf_op jit(solution)/shard_map/while
  51.9 3.4 %copy-start.2 = (f32[16,4,64,64]{3,2,1,0:T(8,128)}, f32[16,4,64,64]{3,2,1,0:T(8,128)S(1)}, u32[]{:S(2)}) copy-start(f32[16,4,64,64]{3,2,1,0:T(8,128)S(1)} %multiply_add_fusion.8) | copy-start | bytes 3145732 | tf_op jit(solution)/shard_map/while
  55.3 8.2 %copy-start.1 = (f32[16,4,64,64]{3,2,1,0:T(8,128)S(1)}, f32[16,4,64,64]{3,2,1,0:T(8,128)}, u32[]{:S(2)}) copy-start(f32[16,4,64,64]{3,2,1,0:T(8,128)} %get-tuple-element.245) | copy-start | bytes 3145732 | tf_op jit(solution)/shard_map/while
  65.1 3.4 %copy-start.2 = (f32[16,4,64,64]{3,2,1,0:T(8,128)}, f32[16,4,64,64]{3,2,1,0:T(8,128)S(1)}, u32[]{:S(2)}) copy-start(f32[16,4,64,64]{3,2,1,0:T(8,128)S(1)} %multiply_add_fusion.8) | copy-start | bytes 3145732 | tf_op jit(solution)/shard_map/while
  68.5 8.2 %copy-start.1 = (f32[16,4,64,64]{3,2,1,0:T(8,128)S(1)}, f32[16,4,64,64]{3,2,1,0:T(8,128)}, u32[]{:S(2)}) copy-start(f32[16,4,64,64]{3,2,1,0:T(8,128)} %get-tuple-element.245) | copy-start | bytes 3145732 | tf_op jit(solution)/shard_map/while
  78.3 3.4 %copy-start.2 = (f32[16,4,64,64]{3,2,1,0:T(8,128)}, f32[16,4,64,64]{3,2,1,0:T(8,128)S(1)}, u32[]{:S(2)}) copy-start(f32[16,4,64,64]{3,2,1,0:T(8,128)S(1)} %multiply_add_fusion.8) | copy-start | bytes 3145732 | tf_op jit(solution)/shard_map/while
  81.7 8.2 %copy-start.1 = (f32[16,4,64,64]{3,2,1,0:T(8,128)S(1)}, f32[16,4,64,64]{3,2,1,0:T(8,128)}, u32[]{:S(2)}) copy-start(f32[16,4,64,64]{3,2,1,0:T(8,128)} %get-tuple-element.245) | copy-start | bytes 3145732 | tf_op jit(solution)/shard_map/while
  91.5 3.4 %copy-start.2 = (f32[16,4,64,64]{3,2,1,0:T(8,128)}, f32[16,4,64,64]{3,2,1,0:T(8,128)S(1)}, u32[]{:S(2)}) copy-start(f32[16,4,64,64]{3,2,1,0:T(8,128)S(1)} %multiply_add_fusion.8) | copy-start | bytes 3145732 | tf_op jit(solution)/shard_map/while
  94.9 8.2 %copy-start.1 = (f32[16,4,64,64]{3,2,1,0:T(8,128)S(1)}, f32[16,4,64,64]{3,2,1,0:T(8,128)}, u32[]{:S(2)}) copy-start(f32[16,4,64,64]{3,2,1,0:T(8,128)} %get-tuple-element.245) | copy-start | bytes 3145732 | tf_op jit(solution)/shard_map/while
  104.7 3.4 %copy-start.2 = (f32[16,4,64,64]{3,2,1,0:T(8,128)}, f32[16,4,64,64]{3,2,1,0:T(8,128)S(1)}, u32[]{:S(2)}) copy-start(f32[16,4,64,64]{3,2,1,0:T(8,128)S(1)} %multiply_add_fusion.8) | copy-start | bytes 3145732 | tf_op jit(solution)/shard_map/while
  108.1 8.2 %copy-start.1 = (f32[16,4,64,64]{3,2,1,0:T(8,128)S(1)}, f32[16,4,64,64]{3,2,1,0:T(8,128)}, u32[]{:S(2)}) copy-start(f32[16,4,64,64]{3,2,1,0:T(8,128)} %get-tuple-element.245) | copy-start | bytes 3145732 | tf_op jit(solution)/shard_map/while
  117.9 3.4 %copy-start.2 = (f32[16,4,64,64]{3,2,1,0:T(8,128)}, f32[16,4,64,64]{3,2,1,0:T(8,128)S(1)}, u32[]{:S(2)}) copy-start(f32[16,4,64,64]{3,2,1,0:T(8,128)S(1)} %multiply_add_fusion.8) | copy-start | bytes 3145732 | tf_op jit(solution)/shard_map/while
  121.3 8.2 %copy-start.1 = (f32[16,4,64,64]{3,2,1,0:T(8,128)S(1)}, f32[16,4,64,64]{3,2,1,0:T(8,128)}, u32[]{:S(2)}) copy-start(f32[16,4,64,64]{3,2,1,0:T(8,128)} %get-tuple-element.245) | copy-start | bytes 3145732 | tf_op jit(solution)/shard_map/while
  131.0 3.4 %copy-start.2 = (f32[16,4,64,64]{3,2,1,0:T(8,128)}, f32[16,4,64,64]{3,2,1,0:T(8,128)S(1)}, u32[]{:S(2)}) copy-start(f32[16,4,64,64]{3,2,1,0:T(8,128)S(1)} %multiply_add_fusion.8) | copy-start | bytes 3145732 | tf_op jit(solution)/shard_map/while
  147.3 40.1 %all-to-all-start = ((f32[16,128,256]{2,1,0:T(8,128)}), f32[16,128,256]{2,1,0:T(8,128)}, u32[]{:S(2)}, u32[]{:S(2)}) async-start(f32[16,128,256]{2,1,0:T(8,128)} %bitcast.113), calls=%async_computation | async-start | bytes 4194304 | tf_op jit(solution)/shard_map/all_to_all | solution.py:19
  155.5 119.1 %all-gather.3.cloned.1.call-start = ((), (), s32[]{:S(2)}) async-start(), calls=%async_computation.4 | async-start | bytes 9437184 | tf_op jit(solution)/shard_map/all_gather | solution.py:219
  206.7 16.9 %copy-start.5 = (s32[16,8]{0,1:T(8,128)S(1)}, s32[16,8]{0,1:T(8,128)}, u32[]{:S(2)}) copy-start(s32[16,8]{0,1:T(8,128)} %param.30) | copy-start | bytes 1540
  282.9 19.5 %copy-start.6 = (s32[16,8]{0,1:T(8,128)S(1)}, s32[16,8]{0,1:T(8,128)}, u32[]{:S(2)}) copy-start(s32[16,8]{0,1:T(8,128)} %param.31) | copy-start | bytes 1540
  284.1 10.1 %all-to-all-start.2 = ((f32[8,3,1024]{2,1,0:T(4,128)}), f32[8,3,1024]{2,1,0:T(4,128)S(1)}, u32[]{:S(2)}, u32[]{:S(2)}) async-start(f32[8,3,1024]{2,1,0:T(4,128)} %broadcast_in_dim.23), calls=%async_computation.2 | async-start | bytes 262144 | tf_op jit(solution)/shard_map/all_to_all | solution.py:37
  295.4 14.6 %all-to-all-start.3 = ((f32[16,3,128]{2,1,0:T(4,128)}), f32[16,3,128]{2,1,0:T(4,128)S(1)}, u32[]{:S(2)}, u32[]{:S(2)}) async-start(f32[16,3,128]{2,1,0:T(4,128)} %broadcast_in_dim.25), calls=%async_computation.3 | async-start | bytes 65536 | tf_op jit(solution)/shard_map/all_to_all | solution.py:37
Sparse Core Ops, SparseCore 0:
  223.6 50.9 all-gather.2
where the time goes:
time: 321 us; the launch traced here: 319 us
  matrix products  84.9 us (26%)
  waiting for transfers between devices  82.3 us (26%)
  blocking collectives  47.1 us (15%)
  local copies, waits for them, and re-layouts  41.7 us (13%)
  other arithmetic  29.1 us (9%)
  starting transfers between devices  19.2 us (6%)
  between operations  14.4 us (4%)
    dot_general x8, matrix products, step(): jnp.einsum('bhij,bhj->bhi', current, unit_now, precision=lax.Precision.HI...  39.5 us
    all_gather x1, waiting for transfers between devices, shards(): lax.all_gather(normed, 'batch', axis=0, tiled=True)  37.6 us
    all_to_all x1, waiting for transfers between devices, sent_and_summed(): parts = lax.all_to_all(in_blocks(x, dim, size), axis, 0, 0, tiled=True)  31 us
    dot_general x8, matrix products, step(): jnp.einsum('bhij,bhj->bhi', current, recept_now, precision=lax.Precision....  26.8 us
    psum x2, blocking collectives, by_axis(): x = lax.psum(x, axis)  17.2 us
    all_to_all x1, blocking collectives, sent_to_all(): return lax.all_to_all(copies, axis, split_axis=0, concat_axis=0, tiled=True)  16.6 us
    all_to_all x2, waiting for transfers between devices, sent_to_all(): return lax.all_to_all(copies, axis, split_axis=0, concat_axis=0, tiled=True)  13.6 us
    all_gather x1, blocking collectives, shards(): lax.all_gather(proposed_tokens_list, 'batch', axis=0, tiled=True)  13.3 us
  transfers between devices with their start and end apart: 4, of which 4 were waited for; matrix products, arithmetic and copies ran while one was open for 0% of the time, Pallas kernels for 0%

commit v1 on v0

--- a/solution.py
+++ b/solution.py
@@ -1,3 +1,4 @@
+import functools
 import math
 import jax
 import jax.numpy as jnp
@@ -7,6 +8,15 @@
 
 HEAD = ("head_0", "head_1")
 HEAD_BATCH = ("head_0", "head_1", "batch")
+
+
+def try_all_gates(s0, axis_name):
+    return jnp.concatenate(
+        lax.all_to_all(jnp.stack([s0] * lax.axis_size(axis_name), axis=0), axis_name, 0, 0), axis=0
+    )
+
+
+_link_slots = functools.partial(try_all_gates, axis_name="batch")
 
 
 def in_blocks(x, dim, size):
@@ -216,7 +226,7 @@
     ).astype(jnp.bfloat16)
     normed = gathered_copies(normed_part, HEAD, 1)
     every, every_ids = (
-        lax.all_gather(normed, "batch", axis=0, tiled=True),
+        _link_slots(normed),
         lax.all_gather(proposed_tokens_list, "batch", axis=0, tiled=True),
     )
     logits = jnp.dot(every, lexicon_projection, preferred_element_type=jnp.float32)

time: 321 us -> 364 us (1.13)
  blocking collectives: 47.1 us -> 134 us
  waiting for transfers between devices: 82.3 us -> 44.6 us
  between operations: 14.4 us -> 1.05 us
  local copies, waits for them, and re-layouts: 41.7 us -> 47.4 us
    all_gather x1, blocking collectives: 13.3 us -> 100 us  [shards(): lax.all_gather(proposed_tokens_list, 'batch', axis=0, tiled=True)]
    all_gather x1 -> x0, waiting for transfers between devices: 37.6 us -> none  [shards(): lax.all_gather(normed, 'batch', axis=0, tiled=True)]
    another operation x0 -> x2, local copies, waits for them, and re-layouts: none -> 5.74 us  [try_all_gates(): jnp.stack([s0] * lax.axis_size(axis_name), axis=0)]
    all_to_all x0 -> x1, starting transfers between devices: none -> 5.09 us  [try_all_gates(): lax.all_to_all(jnp.stack([s0] * lax.axis_size(axis_name), axis=0), axis_n...]
    all_to_all x2, starting transfers between devices: 10.9 us -> 6.86 us  [sent_to_all(): return lax.all_to_all(copies, axis, split_axis=0, concat_axis=0, tiled=True)]
  transfers between devices with their start and end apart: 4 -> 4, of which waited for: 4 -> 3; matrix products, arithmetic and copies ran while one was open for 0% -> 0% of each run, Pallas kernels for 0% -> 0%
where the time goes in v1:
time: 364 us; the launch traced here: 362 us
  blocking collectives  134 us (37%)
  matrix products  84.9 us (23%)
  local copies, waits for them, and re-layouts  47.4 us (13%)
  waiting for transfers between devices  44.6 us (12%)
  other arithmetic  29.1 us (8%)
  starting transfers between devices  20.2 us (6%)
    all_gather x1, blocking collectives, shards(): lax.all_gather(proposed_tokens_list, 'batch', axis=0, tiled=True)  100 us
    dot_general x8, matrix products, step(): jnp.einsum('bhij,bhj->bhi', current, unit_now, precision=lax.Precision.HI...  39.5 us
    all_to_all x1, waiting for transfers between devices, sent_and_summed(): parts = lax.all_to_all(in_blocks(x, dim, size), axis, 0, 0, tiled=True)  31.1 us
    dot_general x8, matrix products, step(): jnp.einsum('bhij,bhj->bhi', current, recept_now, precision=lax.Precision....  26.8 us
    psum x2, blocking collectives, by_axis(): x = lax.psum(x, axis)  17.2 us
    all_to_all x1, blocking collectives, sent_to_all(): return lax.all_to_all(copies, axis, split_axis=0, concat_axis=0, tiled=True)  16.6 us
    all_to_all x2, waiting for transfers between devices, sent_to_all(): return lax.all_to_all(copies, axis, split_axis=0, concat_axis=0, tiled=True)  13.5 us
    add x8, other arithmetic, step(): current * decay_now[:, :, None, :]  12.3 us
  transfers between devices with their start and end apart: 4, of which 3 were waited for; matrix products, arithmetic and copies ran while one was open for 0% of the time, Pallas kernels for 0%

profile of v1, /device:TPU:0, one launch (start us, length us, event | category | flops | bytes accessed | tf_op | source)
XLA Modules:
  0.0 361.8 jit_solution(11618878034084453268)
XLA Ops:
  0.7 3.3 copy.150
  22.4 105.5 %while.12 = (s32[]{:T(128)}, f32[16,4,64,64]{3,2,1,0:T(8,128)}, f32[8,16,4,64]{3,2,1,0:T(4,128)S(1)}, f32[8,16,4,64]{3,2,0,1:T(4,128)}, f32[8,16,4,64]{3,2,1,0:T...) while((s32[]{:T(128)}, f32[16,4,64,64]{3,2,1,0:T(8,128)}, ...), condition=%wide.region_2.3_spmd, body=%wide.region_1.2_spmd.sunk | while | flops 7606274 | bytes 13009081 | solution.py:129
  25.0 4.9 %fusion.54 = f32[16,4,1,64]{3,2,1,0:T(1,128)S(1)} fusion(f32[16,4,64,1]{2,3,1,0:T(1,128)S(1)} %bitcast.119, f32[16,4,64,64]{3,2,1,0:T(8,128)} %get-tuple-element.245), kind=kOutput, calls=%fused_computation.79.clone.1 | convolution fusion | flops 3145728 | bytes 1081344 | tf_op jit(solution)/shard_map/while/body/eval_jaxpr/bhij,bhj->bhi/dot_general | solution.py:120
  32.2 3.3 fusion.55
  38.1 4.9 %fusion.54 = f32[16,4,1,64]{3,2,1,0:T(1,128)S(1)} fusion(f32[16,4,64,1]{2,3,1,0:T(1,128)S(1)} %bitcast.119, f32[16,4,64,64]{3,2,1,0:T(8,128)} %get-tuple-element.245), kind=kOutput, calls=%fused_computation.79.clone.1 | convolution fusion | flops 3145728 | bytes 1081344 | tf_op jit(solution)/shard_map/while/body/eval_jaxpr/bhij,bhj->bhi/dot_general | solution.py:120
  45.4 3.3 fusion.55
  51.3 4.9 %fusion.54 = f32[16,4,1,64]{3,2,1,0:T(1,128)S(1)} fusion(f32[16,4,64,1]{2,3,1,0:T(1,128)S(1)} %bitcast.119, f32[16,4,64,64]{3,2,1,0:T(8,128)} %get-tuple-element.245), kind=kOutput, calls=%fused_computation.79.clone.1 | convolution fusion | flops 3145728 | bytes 1081344 | tf_op jit(solution)/shard_map/while/body/eval_jaxpr/bhij,bhj->bhi/dot_general | solution.py:120
  58.6 3.3 fusion.55
  64.5 4.9 %fusion.54 = f32[16,4,1,64]{3,2,1,0:T(1,128)S(1)} fusion(f32[16,4,64,1]{2,3,1,0:T(1,128)S(1)} %bitcast.119, f32[16,4,64,64]{3,2,1,0:T(8,128)} %get-tuple-element.245), kind=kOutput, calls=%fused_computation.79.clone.1 | convolution fusion | flops 3145728 | bytes 1081344 | tf_op jit(solution)/shard_map/while/body/eval_jaxpr/bhij,bhj->bhi/dot_general | solution.py:120
  71.8 3.3 fusion.55
  77.7 4.9 %fusion.54 = f32[16,4,1,64]{3,2,1,0:T(1,128)S(1)} fusion(f32[16,4,64,1]{2,3,1,0:T(1,128)S(1)} %bitcast.119, f32[16,4,64,64]{3,2,1,0:T(8,128)} %get-tuple-element.245), kind=kOutput, calls=%fused_computation.79.clone.1 | convolution fusion | flops 3145728 | bytes 1081344 | tf_op jit(solution)/shard_map/while/body/eval_jaxpr/bhij,bhj->bhi/dot_general | solution.py:120
  85.0 3.3 fusion.55
  90.9 4.9 %fusion.54 = f32[16,4,1,64]{3,2,1,0:T(1,128)S(1)} fusion(f32[16,4,64,1]{2,3,1,0:T(1,128)S(1)} %bitcast.119, f32[16,4,64,64]{3,2,1,0:T(8,128)} %get-tuple-element.245), kind=kOutput, calls=%fused_computation.79.clone.1 | convolution fusion | flops 3145728 | bytes 1081344 | tf_op jit(solution)/shard_map/while/body/eval_jaxpr/bhij,bhj->bhi/dot_general | solution.py:120
  98.2 3.3 fusion.55
  104.1 4.9 %fusion.54 = f32[16,4,1,64]{3,2,1,0:T(1,128)S(1)} fusion(f32[16,4,64,1]{2,3,1,0:T(1,128)S(1)} %bitcast.119, f32[16,4,64,64]{3,2,1,0:T(8,128)} %get-tuple-element.245), kind=kOutput, calls=%fused_computation.79.clone.1 | convolution fusion | flops 3145728 | bytes 1081344 | tf_op jit(solution)/shard_map/while/body/eval_jaxpr/bhij,bhj->bhi/dot_general | solution.py:120
  111.3 3.3 fusion.55
  117.2 4.9 %fusion.54 = f32[16,4,1,64]{3,2,1,0:T(1,128)S(1)} fusion(f32[16,4,64,1]{2,3,1,0:T(1,128)S(1)} %bitcast.119, f32[16,4,64,64]{3,2,1,0:T(8,128)} %get-tuple-element.245), kind=kOutput, calls=%fused_computation.79.clone.1 | convolution fusion | flops 3145728 | bytes 1081344 | tf_op jit(solution)/shard_map/while/body/eval_jaxpr/bhij,bhj->bhi/dot_general | solution.py:120
  124.5 3.3 fusion.55
  133.4 4.2 %fusion.5 = f32[128,4096]{1,0:T(8,128)} fusion(bf16[256,4096]{1,0:T(8,128)(2,1)S(1)} %copy-done, f32[128,256]{1,0:T(8,128)S(1)} %reshape.131, bf16[128,4096]{1,0:T(8,128)(2,1)S(1)} %copy-done.3, bf16[4096,256]{1,0:T(8,128)(2,1)} %param.21), kind=kOutput, calls=%fused_computation.18 | convolution fusion | flops 537034752 | bytes 7471104 | tf_op jit(solution)/shard_map/dot_general | solution.py:210
  140.8 8.2 %all-to-all-start = ((f32[16,128,256]{2,1,0:T(8,128)}), f32[16,128,256]{2,1,0:T(8,128)}, u32[]{:S(2)}, u32[]{:S(2)}) async-start(f32[16,128,256]{2,1,0:T(8,128)} %bitcast.114), calls=%async_computation | async-start | bytes 4194304 | tf_op jit(solution)/shard_map/all_to_all | solution.py:29
  149.8 31.1 %all-to-all-done = f32[16,128,256]{2,1,0:T(8,128)} async-done(((f32[16,128,256]{2,1,0:T(8,128)}), f32[16,128,256]{2,1,0:T(8,128)}, u32[]{:S(2)}, u32[]{:S(2)}) %all-to-all-start) | async-done | bytes 2097184 | tf_op jit(solution)/shard_map/all_to_all | solution.py:29
  182.7 9.5 %all-reduce.1 = (f32[128]{0:T(128)S(1)}, f32[128]{0:T(128)S(1)}) all-reduce(f32[128]{0:T(128)S(1)} %get-tuple-element.107, f32[128]{0:T(128)S(1)} %get-tuple-element.106), channel_id=1, replica_groups=mesh['head_0'=4,'head_1'=4,'batch'=8] {'head_0'}, use_global_device_ids=true, to_apply=%region_11.12 | all-reduce | flops 256 | bytes 2048 | tf_op jit(solution)/shard_map/psum | solution.py:35
  192.2 7.7 %all-reduce = (f32[128]{0:T(128)S(1)}, f32[128]{0:T(128)S(1)}) all-reduce(f32[128]{0:T(128)S(1)} %get-tuple-element.130, f32[128]{0:T(128)S(1)} %get-tuple-element.131), channel_id=1, replica_groups=mesh['head_0'=4,'head_1'=4,'batch'=8] {'head_1'}, use_global_device_ids=true, to_apply=%region_12.13 | all-reduce | flops 256 | bytes 2048 | tf_op jit(solution)/shard_map/psum | solution.py:35
  200.3 16.6 %all_to_all.25 = bf16[16,128,256]{1,2,0:T(8,128)(2,1)} all-to-all(bf16[16,128,256]{1,2,0:T(8,128)(2,1)S(1)} %broadcast_in_dim.21), channel_id=1, replica_groups=mesh['head_0'=4,'head_1'=4,'batch'=8] {'head_0','head_1'}, dimensions={0} | all-to-all | bytes 2097152 | tf_op jit(solution)/shard_map/all_to_all | solution.py:47
  218.4 4.3 %stack.3 = bf16[8,128,4096]{2,1,0:T(8,128)(2,1)} broadcast(bf16[128,4096]{1,0:T(8,128)(2,1)S(1)} %copy.105), dimensions={1,2} | broadcast | bytes 9437184 | tf_op jit(solution)/shard_map/stack | solution.py:15
  222.7 5.1 %all-to-all-start.2 = ((bf16[8,128,4096]{2,1,0:T(8,128)(2,1)}), bf16[8,128,4096]{2,1,0:T(8,128)(2,1)}, u32[]{:S(2)}, u32[]{:S(2)}) async-start(bf16[8,128,4096]{2,1,0:T(8,128)(2,1)} %stack.3), calls=%async_computation.2 | async-start | bytes 16777216 | tf_op jit(solution)/shard_map/all_to_all | solution.py:15
  227.8 100.4 %all-gather = s32[8,16,8]{1,2,0:T(8,128)S(1)} all-gather(s32[1,16,8]{1,2,0:T(8,128)S(1)} %bitcast.137), channel_id=1, replica_groups=mesh['head_0'=4,'head_1'=4,'batch'=8] {'batch'}, dimensions={0}, use_global_device_ids=true | all-gather | bytes 4608 | tf_op jit(solution)/shard_map/all_gather | solution.py:230
  328.5 8.3 %fusion.23 = (f32[1024]{0:T(1024)S(1)}, f32[1024,512]{0,1:T(8,128)S(1)}) fusion(bf16[1024,4096]{1,0:T(8,128)(2,1)} %bitcast.25, bf16[4096,512]{1,0:T(8,128)(2,1)} %param.29), kind=kOutput, calls=%fused_computation.78 | convolution fusion | flops 4295490560 | bytes 14684160 | tf_op jit(solution)/shard_map/dot_general | solution.py:232
  338.0 3.4 all-to-all-start.3
  341.4 6.1 %all-to-all-done.3 = f32[8,3,1024]{2,1,0:T(4,128)S(1)} async-done(((f32[8,3,1024]{2,1,0:T(4,128)}), f32[8,3,1024]{2,1,0:T(4,128)S(1)}, u32[]{:S(2)}, u32[]{:S(2)}) %all-to-all-start.3) | async-done | bytes 98336 | tf_op jit(solution)/shard_map/all_to_all | solution.py:47
  348.7 3.5 all-to-all-start.4
  352.3 7.5 %all-to-all-done.4 = f32[16,3,128]{2,1,0:T(4,128)S(1)} async-done(((f32[16,3,128]{2,1,0:T(4,128)}), f32[16,3,128]{2,1,0:T(4,128)S(1)}, u32[]{:S(2)}, u32[]{:S(2)}) %all-to-all-start.4) | async-done | bytes 24608 | tf_op jit(solution)/shard_map/all_to_all | solution.py:47
  (199 shorter events, 75.0 us)
Async XLA Ops:
  0.6 132.8 %copy-start = (bf16[256,4096]{1,0:T(8,128)(2,1)S(1)}, bf16[256,4096]{1,0:T(8,128)(2,1)}, u32[]{:S(2)}) copy-start(bf16[256,4096]{1,0:T(8,128)(2,1)} %param.27) | copy-start | bytes 6291460
  0.6 5.1 %copy-start.3 = (bf16[128,4096]{1,0:T(8,128)(2,1)S(1)}, bf16[128,4096]{1,0:T(8,128)(2,1)}, u32[]{:S(2)}) copy-start(bf16[128,4096]{1,0:T(8,128)(2,1)} %param.17) | copy-start | bytes 3145732
  7.8 3.8 %copy-start.7 = (f32[256]{0:T(256)S(1)}, f32[256]{0:T(256)}, u32[]{:S(2)}) copy-start(f32[256]{0:T(256)} %param.24) | copy-start | bytes 3076
  22.4 105.5 %copy-start.4 = (f32[16,8,4]{2,1,0:T(8,128)S(1)}, f32[16,8,4]{2,1,0:T(8,128)}, u32[]{:S(2)}) copy-start(f32[16,8,4]{2,1,0:T(8,128)} %get-tuple-element.108) | copy-start | bytes 6148
  22.4 106.1 %copy-start.8 = (f32[256]{0:T(256)S(1)}, f32[256]{0:T(256)}, u32[]{:S(2)}) copy-start(f32[256]{0:T(256)} %param.25) | copy-start | bytes 3076
  22.4 8.2 %copy-start.1 = (f32[16,4,64,64]{3,2,1,0:T(8,128)S(1)}, f32[16,4,64,64]{3,2,1,0:T(8,128)}, u32[]{:S(2)}) copy-start(f32[16,4,64,64]{3,2,1,0:T(8,128)} %get-tuple-element.245) | copy-start | bytes 3145732 | tf_op jit(solution)/shard_map/while
  32.2 3.4 copy-start.2
  35.6 8.2 %copy-start.1 = (f32[16,4,64,64]{3,2,1,0:T(8,128)S(1)}, f32[16,4,64,64]{3,2,1,0:T(8,128)}, u32[]{:S(2)}) copy-start(f32[16,4,64,64]{3,2,1,0:T(8,128)} %get-tuple-element.245) | copy-start | bytes 3145732 | tf_op jit(solution)/shard_map/while
  45.4 3.4 copy-start.2
  48.8 8.2 %copy-start.1 = (f32[16,4,64,64]{3,2,1,0:T(8,128)S(1)}, f32[16,4,64,64]{3,2,1,0:T(8,128)}, u32[]{:S(2)}) copy-start(f32[16,4,64,64]{3,2,1,0:T(8,128)} %get-tuple-element.245) | copy-start | bytes 3145732 | tf_op jit(solution)/shard_map/while
  58.6 3.4 copy-start.2
  62.0 8.2 %copy-start.1 = (f32[16,4,64,64]{3,2,1,0:T(8,128)S(1)}, f32[16,4,64,64]{3,2,1,0:T(8,128)}, u32[]{:S(2)}) copy-start(f32[16,4,64,64]{3,2,1,0:T(8,128)} %get-tuple-element.245) | copy-start | bytes 3145732 | tf_op jit(solution)/shard_map/while
  71.8 3.4 copy-start.2
  75.2 8.2 %copy-start.1 = (f32[16,4,64,64]{3,2,1,0:T(8,128)S(1)}, f32[16,4,64,64]{3,2,1,0:T(8,128)}, u32[]{:S(2)}) copy-start(f32[16,4,64,64]{3,2,1,0:T(8,128)} %get-tuple-element.245) | copy-start | bytes 3145732 | tf_op jit(solution)/shard_map/while
  85.0 3.4 copy-start.2
  88.4 8.2 %copy-start.1 = (f32[16,4,64,64]{3,2,1,0:T(8,128)S(1)}, f32[16,4,64,64]{3,2,1,0:T(8,128)}, u32[]{:S(2)}) copy-start(f32[16,4,64,64]{3,2,1,0:T(8,128)} %get-tuple-element.245) | copy-start | bytes 3145732 | tf_op jit(solution)/shard_map/while
  98.1 3.4 copy-start.2
  101.5 8.2 %copy-start.1 = (f32[16,4,64,64]{3,2,1,0:T(8,128)S(1)}, f32[16,4,64,64]{3,2,1,0:T(8,128)}, u32[]{:S(2)}) copy-start(f32[16,4,64,64]{3,2,1,0:T(8,128)} %get-tuple-element.245) | copy-start | bytes 3145732 | tf_op jit(solution)/shard_map/while
  111.3 3.4 copy-start.2
  114.7 8.2 %copy-start.1 = (f32[16,4,64,64]{3,2,1,0:T(8,128)S(1)}, f32[16,4,64,64]{3,2,1,0:T(8,128)}, u32[]{:S(2)}) copy-start(f32[16,4,64,64]{3,2,1,0:T(8,128)} %get-tuple-element.245) | copy-start | bytes 3145732 | tf_op jit(solution)/shard_map/while
  124.5 3.4 copy-start.2
  140.8 40.1 %all-to-all-start = ((f32[16,128,256]{2,1,0:T(8,128)}), f32[16,128,256]{2,1,0:T(8,128)}, u32[]{:S(2)}, u32[]{:S(2)}) async-start(f32[16,128,256]{2,1,0:T(8,128)} %bitcast.114), calls=%async_computation | async-start | bytes 4194304 | tf_op jit(solution)/shard_map/all_to_all | solution.py:29
  222.7 5.1 %copy-start.5 = (s32[16,8]{0,1:T(8,128)S(1)}, s32[16,8]{0,1:T(8,128)}, u32[]{:S(2)}) copy-start(s32[16,8]{0,1:T(8,128)} %param.30) | copy-start | bytes 1540
  222.7 105.8 %all-to-all-start.2 = ((bf16[8,128,4096]{2,1,0:T(8,128)(2,1)}), bf16[8,128,4096]{2,1,0:T(8,128)(2,1)}, u32[]{:S(2)}, u32[]{:S(2)}) async-start(bf16[8,128,4096]{2,1,0:T(8,128)(2,1)} %stack.3), calls=%async_computation.2 | async-start | bytes 16777216 | tf_op jit(solution)/shard_map/all_to_all | solution.py:15
  336.8 15.4 %copy-start.6 = (s32[16,8]{0,1:T(8,128)S(1)}, s32[16,8]{0,1:T(8,128)}, u32[]{:S(2)}) copy-start(s32[16,8]{0,1:T(8,128)} %param.31) | copy-start | bytes 1540
  338.0 9.5 %all-to-all-start.3 = ((f32[8,3,1024]{2,1,0:T(4,128)}), f32[8,3,1024]{2,1,0:T(4,128)S(1)}, u32[]{:S(2)}, u32[]{:S(2)}) async-start(f32[8,3,1024]{2,1,0:T(4,128)} %broadcast_in_dim.23), calls=%async_computation.3 | async-start | bytes 262144 | tf_op jit(solution)/shard_map/all_to_all | solution.py:47
  348.7 11.0 %all-to-all-start.4 = ((f32[16,3,128]{2,1,0:T(4,128)}), f32[16,3,128]{2,1,0:T(4,128)S(1)}, u32[]{:S(2)}, u32[]{:S(2)}) async-start(f32[16,3,128]{2,1,0:T(4,128)} %broadcast_in_dim.25), calls=%async_computation.4 | async-start | bytes 65536 | tf_op jit(solution)/shard_map/all_to_all | solution.py:47
